TPU v7x, 32 devices: a whole 2x2x4 slice. The times are simulated.
32 devices in a mesh: walk: 8 (over z, x), chol: 4 (over y, core).
Axes of the slice: x: 2, y: 2, z: 4, core: 2. Of those that a mesh axis runs over, the one named last changes fastest.
Arguments:
- orbitals: bfloat16 [8, 400, 2048], P('walk', None, 'chol'), may hold values from -4 to 4
- intersection_inv: bfloat16 [8, 400, 400], P('walk'), may hold values from -0.18 to 0.18
- interp: bfloat16 [2048, 2048], P(None, 'chol'), may hold values from -0.079549513 to 0.079549513
- occ_interp: bfloat16 [400, 2048], P(None, 'chol'), may hold values from -0.18 to 0.18
- chol_factors: bfloat16 [2048, 2048], P('chol', 'walk'), may hold values from -2 to 2
- fields: float32 [8, 2048], P(None, 'walk'), may hold values from -4 to 4
Outputs:
- new_orbitals: bfloat16 [8, 400, 2048], P('walk', None, 'chol')
- force_bias: float32 [8, 2048], P(None, 'walk')
All inputs are finite; a program needn't handle non-finite values.
Results may differ from a plain program's by a relative error of at most 0.017.
Values may be sent and summed in bfloat16 or wider, within the bound.
A program may use at most 64 MiB of HBM per device.

v0:
```python
import jax
import jax.numpy as jnp
from jax import lax
from jax.sharding import PartitionSpec as P

TERMS = 4
time_root = 2.2


def on_device(orbitals, intersection_inv, interp, occ_interp, chol_factors, fields):
    walkers_here, electrons, basis_here = orbitals.shape
    piece = lax.all_gather(orbitals, "chol", axis=2, tiled=True)
    green = jnp.einsum(
        "wij,wjm->wim", intersection_inv, piece, preferred_element_type=jnp.float32
    ).astype(jnp.bfloat16)
    projected = jnp.einsum("wim,mp->wip", green, interp, preferred_element_type=jnp.float32)
    applied = jnp.einsum("wim,mp->wip", piece, interp, preferred_element_type=jnp.float32)
    projected, current = (projected, applied)
    weights = jnp.sum(occ_interp.astype(jnp.float32)[None] * projected, axis=1)
    factors = chol_factors.astype(jnp.float32)
    all_weights = lax.all_gather(weights, "walk", axis=0, tiled=True)
    partial_bias = jnp.dot(all_weights, factors, precision=lax.Precision.HIGHEST)
    force_bias = lax.psum(partial_bias, "chol")
    coeff = time_root * (fields - force_bias)
    field_part = jnp.dot(coeff, factors.T, precision=lax.Precision.HIGHEST)
    scales = lax.psum_scatter(field_part, "walk", scatter_dimension=0, tiled=True)
    total = orbitals.astype(jnp.float32)
    for order in range(1, TERMS + 1):
        mixed = (current * scales[:, None, :] / order).astype(jnp.bfloat16)
        partial_value = jnp.einsum("wnp,mp->wnm", mixed, interp, preferred_element_type=jnp.float32)
        term_whole = lax.psum(partial_value.astype(jnp.bfloat16), "chol")
        offset = lax.axis_index("chol") * basis_here
        term_local = lax.dynamic_slice_in_dim(term_whole, offset, basis_here, 2)
        total = total + term_local.astype(jnp.float32)
        if order < TERMS:
            current = jnp.einsum(
                "wnm,mp->wnp", term_whole, interp, preferred_element_type=jnp.float32
            )
    return (total.astype(jnp.bfloat16), force_bias)


def solution(mesh):
    placed = (
        P("walk", None, "chol"),
        P("walk", None, None),
        P(None, "chol"),
        P(None, "chol"),
        P("chol", "walk"),
        P(None, "walk"),
    )
    return jax.shard_map(
        on_device,
        mesh=mesh,
        in_specs=placed,
        out_specs=(P("walk", None, "chol"), P(None, "walk")),
        check_vma=False,
    )
```

profile of v0, /device:TPU:0, one launch (start us, length us, event | category | flops | bytes accessed | tf_op | source)
XLA Modules:
  0.0 304.3 jit_solution(10062563972776809825)
XLA Ops:
  7.2 0.0 all-gather.4.cloned.1.call-start
  7.2 0.7 all-gather.4.cloned.1.call-update
  7.9 0.0 all-reduce.6.cloned.1.call-start
  8.0 1.2 dynamic-slice
  9.2 23.1 %all-gather.4.cloned.1.call-done = bf16[1,400,2048]{2,1,0:T(8,128)(2,1)} async-done(((bf16[1,400,512]{2,1,0:T(8,128)(2,1)}), bf16[1,400,2048]{2,1,0:T(8,128)(2,1)}) %all-gather.4.cloned.1.call-update) | async-done | bytes 1638416 | tf_op jit(solution)/shard_map/all_gather | solution.py:12
  32.3 3.5 %fusion.46 = f32[512]{0:T(512)S(1)} fusion(bf16[2048,512]{1,0:T(8,128)(2,1)S(1)} %copy-done, bf16[1,400,2048]{2,1,0:T(8,128)(2,1)} %all-gather.4.cloned.1.call-done, bf16[400,512]{1,0:T(8,128)(2,1)} %param.9, bf16[1,400,400]{2,1,0:T(8,128)(2,1)} %param.7), kind=kOutput, calls=%fused_computation.30 | convolution fusion | flops 1495653888 | bytes 4467200 | tf_op jit(solution)/shard_map/wim,mp->wip/dot_general | solution.py:16
  35.8 26.2 %all-gather.1 = f32[8,1,512]{2,1,0:T(1,128)S(1)} all-gather(f32[1,1,512]{2,1,0:T(1,128)S(1)} %bitcast.75), channel_id=2, replica_groups=mesh['walk'=8,'chol'=4] {'walk'}, dimensions={0}, use_global_device_ids=true | all-gather | bytes 18432 | tf_op jit(solution)/shard_map/all_gather | solution.py:21
  62.0 0.2 fusion.66
  62.2 6.1 %psum.35 = f32[8,256]{1,0:T(8,128)S(1)} all-reduce(f32[8,256]{1,0:T(8,128)S(1)} %fusion.66), channel_id=1, replica_groups=mesh['walk'=8,'chol'=4] {'chol'}, use_global_device_ids=true, to_apply=%region_1.0 | all-reduce | flops 2048 | bytes 16384 | tf_op jit(solution)/shard_map/psum | solution.py:23
  68.3 0.3 fusion.69
  68.6 35.5 %all-reduce = f32[8,512]{1,0:T(8,128)S(1)} all-reduce(f32[8,512]{1,0:T(8,128)S(1)} %fusion.69), channel_id=3, replica_groups=mesh['walk'=8,'chol'=4] {'walk'}, use_global_device_ids=true, to_apply=%region_2.0.clone | all-reduce | flops 4096 | bytes 32768
  104.1 0.6 constant_dynamic-slice_fusion
  104.8 4.5 %fusion = bf16[1,400,2048]{2,1,0:T(8,128)(2,1)} fusion(bf16[2048,512]{1,0:T(8,128)(2,1)S(1)} %copy-done, bf16[1,400,2048]{2,1,0:T(8,128)(2,1)} %all-gather.4.cloned.1.call-done, f32[512]{0:T(512)S(1)} %bitcast.76), kind=kOutput, calls=%fused_computation.5 | convolution fusion | flops 1678950400 | bytes 5376000 | tf_op jit(solution)/shard_map/wnp,mp->wnm/dot_general | solution.py:30
  109.3 0.0 all-reduce.8.cloned.1.call-start
  109.4 40.0 %all-reduce.6.cloned.1.call-done = bf16[1,400,2048]{2,1,0:T(8,128)(2,1)} async-done(((bf16[1,400,2048]{2,1,0:T(8,128)(2,1)}), bf16[1,400,2048]{2,1,0:T(8,128)(2,1)}) %all-reduce.6.cloned.1.call-update) | async-done | bytes 1638416 | tf_op jit(solution)/shard_map/psum | solution.py:31
  149.4 4.5 %fusion.1 = bf16[1,400,2048]{2,1,0:T(8,128)(2,1)} fusion(bf16[2048,512]{1,0:T(8,128)(2,1)S(1)} %copy-done, bf16[1,400,2048]{2,1,0:T(8,128)(2,1)} %all-reduce.6.cloned.1.call-done, f32[512]{0:T(512)S(1)} %bitcast.77), kind=kOutput, calls=%fused_computation.6 | convolution fusion | flops 1679155200 | bytes 5376000 | tf_op jit(solution)/shard_map/wnp,mp->wnm/dot_general | solution.py:30
  153.9 0.0 all-reduce.10.cloned.1.call-start
  154.0 44.1 %all-reduce.8.cloned.1.call-done = bf16[1,400,2048]{2,1,0:T(8,128)(2,1)} async-done(((bf16[1,400,2048]{2,1,0:T(8,128)(2,1)}), bf16[1,400,2048]{2,1,0:T(8,128)(2,1)}) %all-reduce.8.cloned.1.call-update) | async-done | bytes 1638416 | tf_op jit(solution)/shard_map/psum | solution.py:31
  198.0 4.5 %fusion.2 = bf16[1,400,2048]{2,1,0:T(8,128)(2,1)} fusion(bf16[2048,512]{1,0:T(8,128)(2,1)S(1)} %copy-done, bf16[1,400,2048]{2,1,0:T(8,128)(2,1)} %all-reduce.8.cloned.1.call-done, f32[512]{0:T(512)S(1)} %bitcast.78), kind=kOutput, calls=%fused_computation.7 | convolution fusion | flops 1679155200 | bytes 5376000 | tf_op jit(solution)/shard_map/wnp,mp->wnm/dot_general | solution.py:30
  202.6 0.0 all-reduce.12.cloned.1.call-start
  202.6 44.1 %all-reduce.10.cloned.1.call-done = bf16[1,400,2048]{2,1,0:T(8,128)(2,1)} async-done(((bf16[1,400,2048]{2,1,0:T(8,128)(2,1)}), bf16[1,400,2048]{2,1,0:T(8,128)(2,1)}) %all-reduce.10.cloned.1.call-update) | async-done | bytes 1638416 | tf_op jit(solution)/shard_map/psum | solution.py:31
  246.7 4.5 %fusion.3 = bf16[1,400,2048]{2,1,0:T(8,128)(2,1)} fusion(bf16[2048,512]{1,0:T(8,128)(2,1)S(1)} %copy-done, bf16[1,400,2048]{2,1,0:T(8,128)(2,1)} %all-reduce.10.cloned.1.call-done, f32[512]{0:T(512)S(1)} %bitcast.79), kind=kOutput, calls=%fused_computation.8 | convolution fusion | flops 1679155200 | bytes 5376000 | tf_op jit(solution)/shard_map/wnp,mp->wnm/dot_general | solution.py:30
  251.3 44.1 %all-reduce.12.cloned.1.call-done = bf16[1,400,2048]{2,1,0:T(8,128)(2,1)} async-done(((bf16[1,400,2048]{2,1,0:T(8,128)(2,1)}), bf16[1,400,2048]{2,1,0:T(8,128)(2,1)}) %all-reduce.12.cloned.1.call-update) | async-done | bytes 1638416 | tf_op jit(solution)/shard_map/psum | solution.py:31
  295.4 2.4 add_convert_fusion
  (14 shorter events, 0.1 us)
Async XLA Ops:
  7.2 25.1 %copy-start = (bf16[2048,512]{1,0:T(8,128)(2,1)S(1)}, bf16[2048,512]{1,0:T(8,128)(2,1)}, u32[]{:S(2)}) copy-start(bf16[2048,512]{1,0:T(8,128)(2,1)} %param.8) | copy-start | bytes 6291460
  7.2 25.1 %all-gather.4.cloned.1.call-start = ((), (), s32[]{:S(2)}) async-start(), calls=%async_computation | async-start | bytes 2048000 | tf_op jit(solution)/shard_map/all_gather | solution.py:12
  7.9 141.5 %all-reduce.6.cloned.1.call-start = ((), (), s32[]{:S(2)}) async-start(), calls=%async_computation.1 | async-start | bytes 3276800 | tf_op jit(solution)/shard_map/psum | solution.py:31
  9.2 52.8 %copy-start.2 = (bf16[512,256]{1,0:T(8,128)(2,1)S(1)}, bf16[512,256]{1,0:T(8,128)(2,1)}, u32[]{:S(2)}) copy-start(bf16[512,256]{1,0:T(8,128)(2,1)} %param.10) | copy-start | bytes 786436
  9.2 59.1 %copy-start.4 = (f32[8,256]{1,0:T(8,128)S(1)}, f32[8,256]{1,0:T(8,128)}, u32[]{:S(2)}) copy-start(f32[8,256]{1,0:T(8,128)} %param.11) | copy-start | bytes 24580
  68.3 41.0 %copy-start.3 = (f32[8,256]{1,0:T(8,128)}, f32[8,256]{1,0:T(8,128)S(1)}, u32[]{:S(2)}) copy-start(f32[8,256]{1,0:T(8,128)S(1)} %psum.35) | copy-start | bytes 24580
  109.3 88.7 %all-reduce.8.cloned.1.call-start = ((), (), s32[]{:S(2)}) async-start(), calls=%async_computation.2 | async-start | bytes 3276800 | tf_op jit(solution)/shard_map/psum | solution.py:31
  153.9 92.8 %all-reduce.10.cloned.1.call-start = ((), (), s32[]{:S(2)}) async-start(), calls=%async_computation.3 | async-start | bytes 3276800 | tf_op jit(solution)/shard_map/psum | solution.py:31
  202.6 92.8 %all-reduce.12.cloned.1.call-start = ((), (), s32[]{:S(2)}) async-start(), calls=%async_computation.4 | async-start | bytes 3276800 | tf_op jit(solution)/shard_map/psum | solution.py:31
  251.2 44.2 %copy-start.1 = (bf16[1,400,512]{2,1,0:T(8,128)(2,1)S(1)}, bf16[1,400,512]{2,1,0:T(8,128)(2,1)}, u32[]{:S(2)}) copy-start(bf16[1,400,512]{2,1,0:T(8,128)(2,1)} %param.6) | copy-start | bytes 1228804
Sparse Core Ops, SparseCore 0:
  9.5 22.7 all-gather.3
  109.4 39.9 all-reduce.5
  154.0 43.9 all-reduce.7
  202.7 43.9 all-reduce.9
  251.4 43.9 all-reduce.11
where the time goes:
time: 305 us; the launch traced here: 304 us
  waiting for transfers between devices  196 us (64%)
  blocking collectives  67.8 us (22%)
  matrix products  22 us (7%)
  between operations  13.8 us (5%)
    psum x4, waiting for transfers between devices, on_device(): term_whole = lax.psum(partial_value.astype(jnp.bfloat16), 'chol')  172 us
    unnamed x1, blocking collectives  35.5 us
    all_gather x1, blocking collectives, on_device(): all_weights = lax.all_gather(weights, 'walk', axis=0, tiled=True)  26.2 us
    all_gather x1, waiting for transfers between devices, on_device(): piece = lax.all_gather(orbitals, 'chol', axis=2, tiled=True)  23.1 us
    dot_general x4, matrix products, on_device(): jnp.einsum('wnp,mp->wnm', mixed, interp, preferred_element_type=jnp.float32)  18 us
    psum x1, blocking collectives, on_device(): force_bias = lax.psum(partial_bias, 'chol')  6.12 us
  transfers between devices with their start and end apart: 5, of which 5 were waited for; matrix products, arithmetic and copies ran while one was open for 0% of the time, Pallas kernels for 0%

commit v1 on v0

--- a/solution.py
+++ b/solution.py
@@ -28,7 +28,7 @@
     for order in range(1, TERMS + 1):
         mixed = (current * scales[:, None, :] / order).astype(jnp.bfloat16)
         partial_value = jnp.einsum("wnp,mp->wnm", mixed, interp, preferred_element_type=jnp.float32)
-        term_whole = lax.psum(partial_value.astype(jnp.bfloat16), "chol")
+        term_whole = jnp.sum(lax.all_gather(partial_value.astype(jnp.bfloat16), "chol"), axis=0)
         offset = lax.axis_index("chol") * basis_here
         term_local = lax.dynamic_slice_in_dim(term_whole, offset, basis_here, 2)
         total = total + term_local.astype(jnp.float32)

time: 305 us -> 344 us (1.13)
  other arithmetic: 2.4 us -> 25.8 us
  waiting for transfers between devices: 196 us -> 212 us
    all_gather x0 -> x4, waiting for transfers between devices: none -> 188 us  [on_device(): lax.all_gather(partial_value.astype(jnp.bfloat16), 'chol')]
    psum x4 -> x0, waiting for transfers between devices: 172 us -> none  [on_device(): term_whole = lax.psum(partial_value.astype(jnp.bfloat16), 'chol')]
    reduce_sum x0 -> x4, other arithmetic: none -> 23.4 us  [on_device(): jnp.sum(lax.all_gather(partial_value.astype(jnp.bfloat16), 'chol'), axis=0)]
where the time goes in v1:
time: 344 us; the launch traced here: 343 us
  waiting for transfers between devices  212 us (62%)
  blocking collectives  67.8 us (20%)
  other arithmetic  25.8 us (8%)
  matrix products  22.1 us (6%)
  between operations  13.8 us (4%)
    all_gather x4, waiting for transfers between devices, on_device(): lax.all_gather(partial_value.astype(jnp.bfloat16), 'chol')  188 us
    unnamed x1, blocking collectives  35.5 us
    all_gather x1, blocking collectives, on_device(): all_weights = lax.all_gather(weights, 'walk', axis=0, tiled=True)  26.2 us
    reduce_sum x4, other arithmetic, on_device(): jnp.sum(lax.all_gather(partial_value.astype(jnp.bfloat16), 'chol'), axis=0)  23.4 us
    all_gather x1, waiting for transfers between devices, on_device(): piece = lax.all_gather(orbitals, 'chol', axis=2, tiled=True)  23.1 us
    dot_general x4, matrix products, on_device(): jnp.einsum('wnp,mp->wnm', mixed, interp, preferred_element_type=jnp.float32)  18.1 us
  transfers between devices with their start and end apart: 5, of which 5 were waited for; matrix products, arithmetic and copies ran while one was open for 0% of the time, Pallas kernels for 0%

profile of v1, /device:TPU:0, one launch (start us, length us, event | category | flops | bytes accessed | tf_op | source)
XLA Modules:
  0.0 343.4 jit_solution(14299514259871961916)
XLA Ops:
  7.2 0.7 all-gather.12.cloned.1.call-update
  8.0 1.2 dynamic-slice.16
  9.2 23.1 %all-gather.12.cloned.1.call-done = bf16[1,400,2048]{2,1,0:T(8,128)(2,1)} async-done(((bf16[1,400,512]{2,1,0:T(8,128)(2,1)}), bf16[1,400,2048]{2,1,0:T(8,128)(2,1)}) %all-gather.12.cloned.1.call-update) | async-done | bytes 1638416 | tf_op jit(solution)/shard_map/all_gather | solution.py:12
  32.3 3.5 %fusion.15 = f32[512]{0:T(512)S(1)} fusion(bf16[2048,512]{1,0:T(8,128)(2,1)S(1)} %copy-done, bf16[1,400,2048]{2,1,0:T(8,128)(2,1)} %all-gather.12.cloned.1.call-done, bf16[400,512]{1,0:T(8,128)(2,1)} %param.9, bf16[1,400,400]{2,1,0:T(8,128)(2,1)} %param.7), kind=kOutput, calls=%fused_computation.20 | convolution fusion | flops 1495653888 | bytes 4467200 | tf_op jit(solution)/shard_map/wim,mp->wip/dot_general | solution.py:16
  35.8 26.2 %all-gather.5 = f32[8,1,512]{2,1,0:T(1,128)S(1)} all-gather(f32[1,1,512]{2,1,0:T(1,128)S(1)} %bitcast.57), channel_id=2, replica_groups=mesh['walk'=8,'chol'=4] {'walk'}, dimensions={0}, use_global_device_ids=true | all-gather | bytes 18432 | tf_op jit(solution)/shard_map/all_gather | solution.py:21
  62.0 0.2 fusion.30
  62.2 6.1 %psum.7 = f32[8,256]{1,0:T(8,128)S(1)} all-reduce(f32[8,256]{1,0:T(8,128)S(1)} %fusion.30), channel_id=1, replica_groups=mesh['walk'=8,'chol'=4] {'chol'}, use_global_device_ids=true, to_apply=%region_1.0 | all-reduce | flops 2048 | bytes 16384 | tf_op jit(solution)/shard_map/psum | solution.py:23
  68.3 0.3 fusion.33
  68.6 35.5 %all-reduce = f32[8,512]{1,0:T(8,128)S(1)} all-reduce(f32[8,512]{1,0:T(8,128)S(1)} %fusion.33), channel_id=7, replica_groups=mesh['walk'=8,'chol'=4] {'walk'}, use_global_device_ids=true, to_apply=%region_2.0.clone | all-reduce | flops 4096 | bytes 32768
  104.1 0.6 constant_dynamic-slice_fusion
  104.8 4.5 %convolution_convert_fusion.3 = bf16[400,2048]{1,0:T(8,128)(2,1)} fusion(bf16[2048,512]{1,0:T(8,128)(2,1)S(1)} %copy-done, bf16[1,400,2048]{2,1,0:T(8,128)(2,1)} %all-gather.12.cloned.1.call-done, f32[512]{0:T(512)S(1)} %bitcast.58), kind=kOutput, calls=%fused_computation.3 | convolution fusion | flops 1678950400 | bytes 5376000 | tf_op jit(solution)/shard_map/wnp,mp->wnm/dot_general | solution.py:30
  109.4 44.0 %all-gather.14.cloned.1.call-done = bf16[1600,2048]{1,0:T(8,128)(2,1)} async-done(((bf16[400,2048]{1,0:T(8,128)(2,1)}), bf16[1600,2048]{1,0:T(8,128)(2,1)}) %all-gather.14.cloned.1.call-update) | async-done | bytes 6553616 | tf_op jit(solution)/shard_map/all_gather | solution.py:31
  153.3 5.8 %reduce.10 = bf16[400,2048]{1,0:T(8,128)(2,1)} reduce(bf16[4,400,2048]{2,1,0:T(8,128)(2,1)} %bitcast.54, bf16[]{:T(256)} %constant.9.clone.1), dimensions={0}, to_apply=%region_3.0 | reduce | flops 2457600 | bytes 8192002 | tf_op jit(solution)/shard_map/reduce_sum | solution.py:31
  159.1 4.6 %convolution_convert_fusion.2 = bf16[400,2048]{1,0:T(8,128)(2,1)} fusion(bf16[2048,512]{1,0:T(8,128)(2,1)S(1)} %copy-done, bf16[400,2048]{1,0:T(8,128)(2,1)} %reduce.10, f32[512]{0:T(512)S(1)} %bitcast.59), kind=kOutput, calls=%fused_computation.2 | convolution fusion | flops 1679155200 | bytes 5376000 | tf_op jit(solution)/shard_map/wnp,mp->wnm/dot_general | solution.py:30
  163.8 48.0 %all-gather.16.cloned.1.call-done = bf16[1600,2048]{1,0:T(8,128)(2,1)} async-done(((bf16[400,2048]{1,0:T(8,128)(2,1)}), bf16[1600,2048]{1,0:T(8,128)(2,1)}) %all-gather.16.cloned.1.call-update) | async-done | bytes 6553616 | tf_op jit(solution)/shard_map/all_gather | solution.py:31
  211.8 5.9 %reduce.11 = bf16[400,2048]{1,0:T(8,128)(2,1)} reduce(bf16[4,400,2048]{2,1,0:T(8,128)(2,1)} %bitcast.55, bf16[]{:T(256)} %constant.9.clone.1), dimensions={0}, to_apply=%region_4.0 | reduce | flops 2457600 | bytes 8192002 | tf_op jit(solution)/shard_map/reduce_sum | solution.py:31
  217.7 4.5 %convolution_convert_fusion.1 = bf16[400,2048]{1,0:T(8,128)(2,1)} fusion(bf16[2048,512]{1,0:T(8,128)(2,1)S(1)} %copy-done, bf16[400,2048]{1,0:T(8,128)(2,1)} %reduce.11, f32[512]{0:T(512)S(1)} %bitcast.60), kind=kOutput, calls=%fused_computation.1 | convolution fusion | flops 1679155200 | bytes 5376000 | tf_op jit(solution)/shard_map/wnp,mp->wnm/dot_general | solution.py:30
  222.2 0.2 all-gather.20.cloned.1.call-start
  222.4 47.8 %all-gather.18.cloned.1.call-done = bf16[1600,2048]{1,0:T(8,128)(2,1)} async-done(((bf16[400,2048]{1,0:T(8,128)(2,1)}), bf16[1600,2048]{1,0:T(8,128)(2,1)}) %all-gather.18.cloned.1.call-update) | async-done | bytes 6553616 | tf_op jit(solution)/shard_map/all_gather | solution.py:31
  270.2 5.8 %reduce.12 = bf16[400,2048]{1,0:T(8,128)(2,1)} reduce(bf16[4,400,2048]{2,1,0:T(8,128)(2,1)} %bitcast.56, bf16[]{:T(256)} %constant.9.clone.1), dimensions={0}, to_apply=%region_5.0 | reduce | flops 2457600 | bytes 8192002 | tf_op jit(solution)/shard_map/reduce_sum | solution.py:31
  276.0 4.5 %convolution_convert_fusion = bf16[400,2048]{1,0:T(8,128)(2,1)} fusion(bf16[2048,512]{1,0:T(8,128)(2,1)S(1)} %copy-done, bf16[400,2048]{1,0:T(8,128)(2,1)} %reduce.12, f32[512]{0:T(512)S(1)} %bitcast.61), kind=kOutput, calls=%fused_computation | convolution fusion | flops 1679155200 | bytes 5376000 | tf_op jit(solution)/shard_map/wnp,mp->wnm/dot_general | solution.py:30
  280.6 48.0 %all-gather.20.cloned.1.call-done = bf16[1600,2048]{1,0:T(8,128)(2,1)} async-done(((bf16[400,2048]{1,0:T(8,128)(2,1)}), bf16[1600,2048]{1,0:T(8,128)(2,1)}) %all-gather.20.cloned.1.call-update) | async-done | bytes 6553616 | tf_op jit(solution)/shard_map/all_gather | solution.py:31
  328.6 5.9 %reduce.13 = bf16[400,2048]{1,0:T(8,128)(2,1)} reduce(bf16[4,400,2048]{2,1,0:T(8,128)(2,1)} %bitcast.53, bf16[]{:T(256)} %constant.9.clone.1), dimensions={0}, to_apply=%region_6.0 | reduce | flops 2457600 | bytes 8192002 | tf_op jit(solution)/shard_map/reduce_sum | solution.py:31
  334.4 2.4 fusion.18
  (18 shorter events, 0.3 us)
Async XLA Ops:
  7.2 25.1 %copy-start = (bf16[2048,512]{1,0:T(8,128)(2,1)S(1)}, bf16[2048,512]{1,0:T(8,128)(2,1)}, u32[]{:S(2)}) copy-start(bf16[2048,512]{1,0:T(8,128)(2,1)} %param.8) | copy-start | bytes 6291460
  7.2 25.1 %all-gather.12.cloned.1.call-start = ((), (), s32[]{:S(2)}) async-start(), calls=%async_computation | async-start | bytes 2048000 | tf_op jit(solution)/shard_map/all_gather | solution.py:12
  7.9 145.4 %all-gather.14.cloned.1.call-start = ((), (), s32[]{:S(2)}) async-start(), calls=%async_computation.1 | async-start | bytes 8192000 | tf_op jit(solution)/shard_map/all_gather | solution.py:31
  9.2 52.8 %copy-start.2 = (bf16[512,256]{1,0:T(8,128)(2,1)S(1)}, bf16[512,256]{1,0:T(8,128)(2,1)}, u32[]{:S(2)}) copy-start(bf16[512,256]{1,0:T(8,128)(2,1)} %param.10) | copy-start | bytes 786436
  9.2 59.1 %copy-start.4 = (f32[8,256]{1,0:T(8,128)S(1)}, f32[8,256]{1,0:T(8,128)}, u32[]{:S(2)}) copy-start(f32[8,256]{1,0:T(8,128)} %param.11) | copy-start | bytes 24580
  68.3 41.0 %copy-start.3 = (f32[8,256]{1,0:T(8,128)}, f32[8,256]{1,0:T(8,128)S(1)}, u32[]{:S(2)}) copy-start(f32[8,256]{1,0:T(8,128)S(1)} %psum.7) | copy-start | bytes 24580
  109.3 102.4 %all-gather.16.cloned.1.call-start = ((), (), s32[]{:S(2)}) async-start(), calls=%async_computation.2 | async-start | bytes 8192000 | tf_op jit(solution)/shard_map/all_gather | solution.py:31
  163.8 106.4 %all-gather.18.cloned.1.call-start = ((), (), s32[]{:S(2)}) async-start(), calls=%async_computation.3 | async-start | bytes 8192000 | tf_op jit(solution)/shard_map/all_gather | solution.py:31
  222.2 106.4 %all-gather.20.cloned.1.call-start = ((), (), s32[]{:S(2)}) async-start(), calls=%async_computation.4 | async-start | bytes 8192000 | tf_op jit(solution)/shard_map/all_gather | solution.py:31
  328.6 5.9 %copy-start.1 = (bf16[1,400,512]{2,1,0:T(8,128)(2,1)S(1)}, bf16[1,400,512]{2,1,0:T(8,128)(2,1)}, u32[]{:S(2)}) copy-start(bf16[1,400,512]{2,1,0:T(8,128)(2,1)} %param.6) | copy-start | bytes 1228804
Sparse Core Ops, SparseCore 0:
  9.5 22.7 all-gather.11
  109.4 43.8 all-gather.13
  163.9 47.8 all-gather.15
  222.3 47.8 all-gather.17
  280.7 47.8 all-gather.19
